TPU v7x, 32 devices: a whole 2x2x4 slice. The times are simulated.
32 devices in a mesh: pipe: 2 (over x), tensor: 4 (over y, core), seq: 4 (over z).
Axes of the slice: x: 2, y: 2, z: 4, core: 2. Of those that a mesh axis runs over, the one named last changes fastest.
Arguments:
- tokens: bfloat16 [2, 512, 2560], P(None, 'seq', 'tensor'), may hold values from -6 to 6
- prenorm_gain: float32 [2, 2560], P('pipe'), may hold values from 0.5 to 1.5
- gate_weight: bfloat16 [2, 2560, 5120], P('pipe', None, 'tensor'), may hold values from -0.125 to 0.125
- inner_weight: bfloat16 [2, 2560, 5120], P('pipe', None, 'tensor'), may hold values from -0.125 to 0.125
- state_weight: bfloat16 [2, 2560, 256], P('pipe'), may hold values from -0.125 to 0.125
- step_weight: bfloat16 [2, 2560, 80], P('pipe', None, 'tensor'), may hold values from -0.125 to 0.125
- inner_taps: float32 [2, 5, 5120], P('pipe', None, 'tensor'), may hold values from -3 to 3
- state_taps: float32 [2, 5, 256], P('pipe'), may hold values from -3 to 3
- step_bias: float32 [2, 80], P('pipe', 'tensor'), may hold values from -5 to -2
- decay_rate: float32 [2, 80], P('pipe', 'tensor'), may hold values from 0.001953125 to 1
- skip_scale: float32 [2, 80], P('pipe', 'tensor'), may hold values from 0.5 to 1.5
- inner_gain: float32 [2, 5120], P('pipe', 'tensor'), may hold values from 0.5 to 1.5
- out_weight: bfloat16 [2, 5120, 2560], P('pipe', 'tensor'), may hold values from -0.078125 to 0.078125
Outputs:
- layer_outputs: bfloat16 [2, 2, 512, 2560], P('pipe', None, 'seq', 'tensor')
All inputs are finite; a program needn't handle non-finite values.
Results may differ from a plain program's by a relative error of at most 0.019.
Values may be sent and summed in bfloat16 or wider, within the bound.
A program may use at most 64 MiB of HBM per device.

v0:
```python
import jax
import jax.numpy as jnp
from jax import lax
from jax.sharding import PartitionSpec as P

BLOCK = 128
INNER = 5120
EPS = 1e-05


def shifted(value, axis, steps):
    count = lax.axis_size(axis)
    first, last = (max(0, -steps), min(count, count - steps))
    return lax.ppermute(value, axis, [(source, source + steps) for source in range(first, last)])


def prefix(array, axis, join, neutral):
    place = lax.axis_index(axis)
    gathered = jax.tree.map(
        lambda a, kind: lax.all_gather(a.astype(kind), axis), array, (jnp.bfloat16, jnp.bfloat16)
    )
    state = jax.tree.map(lambda a, e: jnp.zeros_like(a) + jnp.asarray(e, a.dtype), array, neutral)

    def one(hop, state):
        return join(
            state,
            jax.tree.map(
                lambda a, own: lax.dynamic_index_in_dim(a, hop, 0, False).astype(own.dtype),
                gathered,
                array,
            ),
        )

    return lax.fori_loop(0, place, one, state)


def causal_taps(rim, values, taps):
    width = taps.shape[0] - 1
    length = values.shape[0]
    padded = jnp.concatenate([rim, values], axis=0).astype(jnp.float32)
    total = jnp.broadcast_to(taps[width][None, :], (length, values.shape[1]))
    for index in range(width):
        total = total + taps[index][None, :] * padded[index : index + length]
    return jax.nn.silu(total).astype(jnp.bfloat16)


def fold_states(carried, items):
    decay_acc, state_acc = carried
    decay, state = items
    return ((decay_acc * decay, state_acc * decay[:, None, None] + state), (decay_acc, state_acc))


def combine_states(earlier, later):
    return (earlier[0] * later[0], earlier[1] * later[0][:, None, None] + later[1])


def mixer(current, weights):
    (
        prenorm,
        gate_weight,
        inner_weight,
        state_weight,
        step_weight,
        inner_taps,
        state_taps,
        step_bias,
        decay_rate,
        skip_scale,
        inner_gain,
        out_weight,
    ) = weights
    rows = current.shape[0]
    widened = current.astype(jnp.float32)
    normed_in = (
        widened * lax.rsqrt(jnp.mean(widened * widened, axis=1, keepdims=True) + EPS) * prenorm
    ).astype(jnp.bfloat16)
    gate_raw = jnp.dot(normed_in, gate_weight, preferred_element_type=jnp.float32).astype(
        jnp.bfloat16
    )
    inner_raw = jnp.dot(normed_in, inner_weight, preferred_element_type=jnp.float32).astype(
        jnp.bfloat16
    )
    state_raw = jnp.dot(normed_in, state_weight, preferred_element_type=jnp.float32).astype(
        jnp.bfloat16
    )
    step_raw = jnp.dot(normed_in, step_weight, preferred_element_type=jnp.float32)
    inner_width = inner_raw.shape[1]
    reach = inner_taps.shape[0] - 2
    rim = shifted(
        jnp.concatenate([inner_raw[rows - reach :], state_raw[rows - reach :]], axis=1), "seq", 1
    )
    inner_conv = causal_taps(rim[:, :inner_width], inner_raw, inner_taps)
    state_conv = causal_taps(rim[:, inner_width:], state_raw, state_taps)
    heads = step_bias.shape[0]
    head_size = inner_width // heads
    state_size = state_raw.shape[1] // 2
    blocks = rows // BLOCK
    step_size = jax.nn.softplus(step_raw + step_bias)
    step_blocks = step_size.reshape(blocks, BLOCK, heads)
    cumulative = jnp.cumsum(-step_blocks * decay_rate, axis=1)
    inner_blocks = inner_conv.reshape(blocks, BLOCK, heads, head_size)
    input_blocks = state_conv[:, :state_size].reshape(blocks, BLOCK, state_size)
    output_blocks = state_conv[:, state_size:].reshape(blocks, BLOCK, state_size)
    weighting = jnp.exp(cumulative[:, -1:, :] - cumulative) * step_blocks
    weighted = (inner_blocks.astype(jnp.float32) * weighting[..., None]).astype(jnp.bfloat16)
    states = jnp.einsum(
        "bshp,bsn->bhpn", weighted, input_blocks, preferred_element_type=jnp.float32
    )
    decays = jnp.exp(cumulative[:, -1, :])
    start = (
        jnp.ones((heads,), jnp.float32),
        jnp.zeros((heads, head_size, state_size), jnp.float32),
    )
    (device_decay, device_state), (prior_decay, prior_state) = lax.scan(
        fold_states, start, (decays, states)
    )
    entry_decay, entry_state = prefix(
        (device_decay, device_state),
        "seq",
        combine_states,
        (jnp.ones_like(device_decay), jnp.zeros_like(device_state)),
    )
    scores = jnp.einsum(
        "bqn,bsn->bqs", output_blocks, input_blocks, preferred_element_type=jnp.float32
    )
    by_head = jnp.transpose(cumulative, (0, 2, 1))
    later = lax.broadcasted_iota(jnp.int32, (BLOCK, BLOCK), 0) >= lax.broadcasted_iota(
        jnp.int32, (BLOCK, BLOCK), 1
    )
    decay = jnp.exp(jnp.where(later, by_head[:, :, :, None] - by_head[:, :, None, :], -jnp.inf))
    mixing = (
        scores[:, None] * decay * jnp.transpose(step_blocks, (0, 2, 1))[:, :, None, :]
    ).astype(jnp.bfloat16)
    inside = jnp.einsum("bhqs,bshp->bqhp", mixing, inner_blocks, preferred_element_type=jnp.float32)
    entering = prior_state + prior_decay[:, :, None, None] * entry_state[None]
    across = jnp.exp(cumulative)[..., None] * jnp.einsum(
        "bqn,bhpn->bqhp",
        output_blocks.astype(jnp.float32),
        entering,
        precision=lax.Precision.HIGHEST,
    )
    mixed = inside + across + skip_scale[None, None, :, None] * inner_blocks.astype(jnp.float32)
    mixed = mixed.reshape(rows, inner_width)
    gated = mixed * jax.nn.silu(gate_raw.astype(jnp.float32))
    squares = lax.psum(jnp.sum(gated * gated, axis=1), "tensor")
    normed = (gated * lax.rsqrt(squares / INNER + EPS)[:, None] * inner_gain).astype(jnp.bfloat16)
    return jnp.dot(normed, out_weight, preferred_element_type=jnp.float32)


def shards(
    tokens,
    prenorm_gain,
    gate_weight,
    inner_weight,
    state_weight,
    step_weight,
    inner_taps,
    state_taps,
    step_bias,
    decay_rate,
    skip_scale,
    inner_gain,
    out_weight,
):
    weights = (
        prenorm_gain[0],
        gate_weight[0],
        inner_weight[0],
        state_weight[0],
        step_weight[0],
        inner_taps[0],
        state_taps[0],
        step_bias[0],
        decay_rate[0],
        skip_scale[0],
        inner_gain[0],
        out_weight[0],
    )
    sections = lax.axis_size("pipe")
    section = lax.axis_index("pipe")
    share = lax.axis_size("tensor")
    member = lax.axis_index("tensor")
    all_tokens = lax.all_gather(tokens, "tensor", axis=2, tiled=True)
    micro_count, rows, width = all_tokens.shape
    narrow = width // share
    outputs = jnp.zeros((micro_count, rows, narrow), jnp.bfloat16)
    carried = None
    rounds = micro_count + sections - 1
    for turn in range(rounds):
        fresh = all_tokens[min(turn, micro_count - 1)]
        if turn == 0:
            current = fresh
        else:
            incoming = lax.all_gather(carried, "tensor", axis=1, tiled=True)
            current = jnp.where(section == 0, fresh, incoming)
        term = mixer(current, weights)
        summed = lax.psum_scatter(
            term.astype(jnp.bfloat16), "tensor", scatter_dimension=1, tiled=True
        ).astype(jnp.float32)
        base = lax.dynamic_slice_in_dim(current, member * narrow, narrow, 1)
        own = (base.astype(jnp.float32) + summed).astype(jnp.bfloat16)
        micro = turn - section
        valid = jnp.logical_and(micro >= 0, micro < micro_count)
        position = jnp.clip(micro, 0, micro_count - 1)
        previous = lax.dynamic_index_in_dim(outputs, position, 0, keepdims=False)
        outputs = lax.dynamic_update_index_in_dim(
            outputs, jnp.where(valid, own, previous), position, 0
        )
        if turn + 1 < rounds:
            carried = shifted(own, "pipe", 1)
    return outputs[None]


def solution(mesh):
    placed = (
        P(None, "seq", "tensor"),
        P("pipe", None),
        P("pipe", None, "tensor"),
        P("pipe", None, "tensor"),
        P("pipe", None, None),
        P("pipe", None, "tensor"),
        P("pipe", None, "tensor"),
        P("pipe", None, None),
        P("pipe", "tensor"),
        P("pipe", "tensor"),
        P("pipe", "tensor"),
        P("pipe", "tensor"),
        P("pipe", "tensor", None),
    )
    return jax.shard_map(
        shards,
        mesh=mesh,
        in_specs=placed,
        out_specs=P("pipe", None, "seq", "tensor"),
        check_vma=False,
    )
```

profile of v0, /device:TPU:0, one launch (start us, length us, event | category | flops | bytes accessed | tf_op | source)
XLA Modules:
  0.0 362.3 jit_solution(9276554146936817338)
XLA Ops:
  8.0 0.8 slice_reduce_fusion.4
  9.6 20.2 %all-gather.11.cloned.1.call-done = bf16[2,128,2560]{2,1,0:T(8,128)(2,1)} async-done(((bf16[2,128,640]{2,1,0:T(8,128)(2,1)}), bf16[2,128,2560]{2,1,0:T(8,128)(2,1)}) %all-gather.11.cloned.1.call-update) | async-done | bytes 1310736 | tf_op jit(solution)/shard_map/all_gather | solution.py:183
  29.8 1.4 fusion.54
  31.2 1.5 compare_select_fusion.2
  33.8 3.9 %fusion.27 = bf16[128,1280]{1,0:T(8,128)(2,1)S(1)} fusion(bf16[1,2560,1280]{2,1,0:T(8,128)(2,1)} %param.22, f32[2560]{0:T(1024)S(1)} %reduce.3, f32[128]{0:T(128)S(1)} %add_rsqrt_fusion.5, bf16[2,128,2560]{2,1,0:T(8,128)(2,1)S(1)} %copy-done.1), kind=kOutput, calls=%fused_computation.27 | convolution fusion | flops 840335360 | bytes 7549440 | tf_op jit(solution)/shard_map/dot_general | solution.py:80
  39.1 3.4 collective-permute-start
  42.6 1.1 copy.73
  44.1 1.0 maximum_convert_fusion
  45.1 1.2 multiply_convert_fusion.13
  46.3 1.2 copy.74
  47.7 1.0 fusion.78
  48.8 11.7 %all-gather = bf16[4,1,20]{2,1,0:T(2,128)(2,1)S(1)} all-gather(bf16[1,1,20]{2,1,0:T(2,128)(2,1)S(1)} %copy-done.25), channel_id=2, replica_groups=mesh['pipe'=2,'tensor'=4,'seq'=4] {'seq'}, dimensions={0}, use_global_device_ids=true | all-gather | bytes 200 | tf_op jit(solution)/shard_map/all_gather | solution.py:20
  60.5 1.0 copy.75
  61.6 0.9 copy.68
  62.6 19.5 %all-gather.13.cloned.1.call-done = bf16[80,64,128]{2,1,0:T(8,128)(2,1)} async-done(((bf16[20,64,128]{2,1,0:T(8,128)(2,1)}), bf16[80,64,128]{2,1,0:T(8,128)(2,1)}) %all-gather.13.cloned.1.call-update) | async-done | bytes 1310736 | tf_op jit(solution)/shard_map/all_gather | solution.py:20
  84.1 1.1 copy.76
  85.2 5.0 %multiply_reduce_fusion.2 = (f32[128]{0:T(128)S(1)}, f32[128,1280]{1,0:T(8,128)}) fusion(f32[128,1280]{1,0:T(8,128)} %copy.76, bf16[1,2560,1280]{2,1,0:T(8,128)(2,1)} %param.21, f32[2560]{0:T(1024)S(1)} %reduce.3, f32[128]{0:T(128)S(1)} %copy-done.22, bf16[2,128,2560]{2,1,0:T(8,128)(2,1)S(1)} %copy-done.1), kind=kOutput, calls=%fused_computation.132 | convolution fusion | flops 841645952 | bytes 8532992 | tf_op jit(solution)/shard_map/dot_general | solution.py:77
  90.1 5.8 %psum.21 = f32[128]{0:T(128)S(1)} all-reduce(f32[128]{0:T(128)S(1)} %get-tuple-element.269), channel_id=1, replica_groups=mesh['pipe'=2,'tensor'=4,'seq'=4] {'tensor'}, use_global_device_ids=true, to_apply=%region_5.6 | all-reduce | flops 128 | bytes 1024 | tf_op jit(solution)/shard_map/psum | solution.py:145
  96.0 4.2 %fusion.18 = bf16[128,2560]{1,0:T(8,128)(2,1)S(1)} fusion(bf16[1,1280,2560]{2,1,0:T(8,128)(2,1)} %param.31, f32[128,1280]{1,0:T(8,128)} %get-tuple-element.270, f32[1280]{0:T(1024)S(1)} %reduce.7, f32[128]{0:T(128)S(1)} %add_rsqrt_fusion.4), kind=kOutput, calls=%fused_computation.24 | convolution fusion | flops 839680000 | bytes 7869952 | tf_op jit(solution)/shard_map/dot_general | solution.py:147
  100.1 1.1 copy.95
  101.3 25.3 %reduce-scatter.10.cloned.1.call-done = bf16[640,128]{1,0:T(8,128)(2,1)} async-done(((bf16[2560,128]{1,0:T(8,128)(2,1)}), bf16[640,128]{1,0:T(8,128)(2,1)}) %reduce-scatter.10.cloned.1.call-update) | async-done | bytes 163856
  126.6 1.1 copy.96
  129.2 3.4 collective-permute-start.1
  132.6 3.6 collective-permute-done.1
  136.2 6.9 %all_gather.36 = bf16[128,2560]{1,0:T(8,128)(2,1)S(1)} all-gather(bf16[128,640]{1,0:T(8,128)(2,1)S(1)} %collective-permute-done.1), channel_id=1, replica_groups=mesh['pipe'=2,'tensor'=4,'seq'=4] {'tensor'}, dimensions={1}, use_global_device_ids=true | all-gather | bytes 819200 | tf_op jit(solution)/shard_map/all_gather | solution.py:194
  143.9 4.0 %fusion.30 = bf16[128,1280]{1,0:T(8,128)(2,1)S(1)} fusion(bf16[1,2560,1280]{2,1,0:T(8,128)(2,1)} %param.22, bf16[128,2560]{1,0:T(8,128)(2,1)S(1)} %get-tuple-element.247, f32[2560]{0:T(1024)S(1)} %reduce.3, f32[128]{0:T(128)S(1)} %add_rsqrt_fusion.3), kind=kOutput, calls=%fused_computation.28 | convolution fusion | flops 840335360 | bytes 7547392 | tf_op jit(solution)/shard_map/dot_general | solution.py:80
  149.9 4.0 %collective-permute-start.2 = (bf16[3,1536]{1,0:T(4,128)(2,1)}, bf16[3,1536]{1,0:T(4,128)(2,1)}, u32[]{:S(2)}, u32[]{:S(2)}) collective-permute-start(bf16[3,1536]{1,0:T(4,128)(2,1)} %pad_maximum_fusion.1), channel_id=1, source_target_pairs={{0,1},{1,2},{2,3},{4,5},{5,6},{6,7},{8,9},{9,10},{10,11},{12,13},{... | collective-permute-start | bytes 27656 | tf_op jit(solution)/shard_map/ppermute | solution.py:14
  154.1 1.1 copy.82
  155.2 0.8 slice.286
  156.7 1.0 maximum_convert_fusion.1
  157.8 1.2 multiply_convert_fusion.10
  159.0 1.2 copy.83
  160.2 1.0 fusion.79
  161.2 11.7 %all-gather.2 = bf16[4,1,20]{2,1,0:T(2,128)(2,1)S(1)} all-gather(bf16[1,1,20]{2,1,0:T(2,128)(2,1)S(1)} %copy-done.26), channel_id=4, replica_groups=mesh['pipe'=2,'tensor'=4,'seq'=4] {'seq'}, dimensions={0}, use_global_device_ids=true | all-gather | bytes 200 | tf_op jit(solution)/shard_map/all_gather | solution.py:20
  173.0 1.1 copy.84
  174.0 0.9 copy.77
  175.0 21.2 %all-gather.15.cloned.1.call-done = bf16[80,64,128]{2,1,0:T(8,128)(2,1)} async-done(((bf16[20,64,128]{2,1,0:T(8,128)(2,1)}), bf16[80,64,128]{2,1,0:T(8,128)(2,1)}) %all-gather.15.cloned.1.call-update) | async-done | bytes 1310736 | tf_op jit(solution)/shard_map/all_gather | solution.py:20
  197.5 1.5 fusion.76
  199.1 2.2 copy.85
  201.3 5.0 %multiply_reduce_fusion.1 = (f32[128]{0:T(128)S(1)}, f32[128,1280]{1,0:T(8,128)}) fusion(f32[128,1280]{1,0:T(8,128)} %copy.85, bf16[1,2560,1280]{2,1,0:T(8,128)(2,1)} %param.21, bf16[128,2560]{1,0:T(8,128)(2,1)S(1)} %copy-done.5, f32[2560]{0:T(1024)S(1)} %reduce.3, f32[128]{0:T(128)S(1)} %copy-done.24), kind=kOutput, calls=%fused_computation.123 | convolution fusion | flops 841645952 | bytes 8530944 | tf_op jit(solution)/shard_map/dot_general | solution.py:77
  206.3 5.8 %psum.22 = f32[128]{0:T(128)S(1)} all-reduce(f32[128]{0:T(128)S(1)} %get-tuple-element.271), channel_id=1, replica_groups=mesh['pipe'=2,'tensor'=4,'seq'=4] {'tensor'}, use_global_device_ids=true, to_apply=%region_12.13 | all-reduce | flops 128 | bytes 1024 | tf_op jit(solution)/shard_map/psum | solution.py:145
  212.1 5.0 %fusion.21 = bf16[128,2560]{1,0:T(8,128)(2,1)} fusion(bf16[1,1280,2560]{2,1,0:T(8,128)(2,1)} %param.31, f32[128,1280]{1,0:T(8,128)} %get-tuple-element.272, f32[128]{0:T(128)S(1)} %add_rsqrt_fusion.2, f32[1280]{0:T(1024)S(1)} %reduce.7), kind=kOutput, calls=%fused_computation.25 | convolution fusion | flops 839680000 | bytes 7869952 | tf_op jit(solution)/shard_map/dot_general | solution.py:147
  217.1 2.2 copy.97
  219.4 0.9 constant_dynamic-slice_fusion
  220.3 24.4 %reduce-scatter.12.cloned.1.call-done = bf16[640,128]{1,0:T(8,128)(2,1)} async-done(((bf16[2560,128]{1,0:T(8,128)(2,1)}), bf16[640,128]{1,0:T(8,128)(2,1)}) %reduce-scatter.12.cloned.1.call-update) | async-done | bytes 163856
  244.7 1.7 copy.98
  246.4 1.6 bitcast_dynamic-update-slice_fusion
  248.1 3.3 collective-permute-start.3
  251.5 3.3 collective-permute-done.3
  254.8 6.9 %all_gather.39 = bf16[128,2560]{1,0:T(8,128)(2,1)S(1)} all-gather(bf16[128,640]{1,0:T(8,128)(2,1)S(1)} %collective-permute-done.3), channel_id=1, replica_groups=mesh['pipe'=2,'tensor'=4,'seq'=4] {'tensor'}, dimensions={1}, use_global_device_ids=true | all-gather | bytes 819200 | tf_op jit(solution)/shard_map/all_gather | solution.py:194
  262.4 4.0 %fusion.33 = bf16[128,1280]{1,0:T(8,128)(2,1)S(1)} fusion(bf16[1,2560,1280]{2,1,0:T(8,128)(2,1)} %param.22, bf16[128,2560]{1,0:T(8,128)(2,1)S(1)} %get-tuple-element.241, f32[128]{0:T(128)S(1)} %add_rsqrt_fusion.1, f32[2560]{0:T(1024)S(1)} %reduce.3), kind=kOutput, calls=%fused_computation.29 | convolution fusion | flops 840335360 | bytes 7547392 | tf_op jit(solution)/shard_map/dot_general | solution.py:80
  267.4 3.4 collective-permute-start.4
  271.2 1.0 collective-permute-done.4
  273.1 1.0 fusion.80
  274.1 11.7 %all-gather.4 = bf16[4,1,20]{2,1,0:T(2,128)(2,1)S(1)} all-gather(bf16[1,1,20]{2,1,0:T(2,128)(2,1)S(1)} %get-tuple-element.253), channel_id=6, replica_groups=mesh['pipe'=2,'tensor'=4,'seq'=4] {'seq'}, dimensions={0}, use_global_device_ids=true | all-gather | bytes 200 | tf_op jit(solution)/shard_map/all_gather | solution.py:20
  286.1 0.9 copy.86
  287.1 22.4 %all-gather.17.cloned.1.call-done = bf16[80,64,128]{2,1,0:T(8,128)(2,1)} async-done(((bf16[20,64,128]{2,1,0:T(8,128)(2,1)}), bf16[80,64,128]{2,1,0:T(8,128)(2,1)}) %all-gather.17.cloned.1.call-update) | async-done | bytes 1310736 | tf_op jit(solution)/shard_map/all_gather | solution.py:20
  311.5 0.8 copy-done.3
  312.3 4.9 %multiply_reduce_fusion = (f32[128]{0:T(128)S(1)}, f32[128,1280]{1,0:T(8,128)}) fusion(f32[128,1280]{1,0:T(8,128)S(1)} %copy.94, bf16[1,2560,1280]{2,1,0:T(8,128)(2,1)} %param.21, bf16[128,2560]{1,0:T(8,128)(2,1)S(1)} %copy-done.3, f32[128]{0:T(128)S(1)} %copy-done.20, f32[2560]{0:T(1024)S(1)} %reduce.3), kind=kOutput, calls=%fused_computation.114 | convolution fusion | flops 841645952 | bytes 8530944 | tf_op jit(solution)/shard_map/dot_general | solution.py:77
  317.2 5.8 %psum.23 = f32[128]{0:T(128)S(1)} all-reduce(f32[128]{0:T(128)S(1)} %get-tuple-element.273), channel_id=1, replica_groups=mesh['pipe'=2,'tensor'=4,'seq'=4] {'tensor'}, use_global_device_ids=true, to_apply=%region_19.20 | all-reduce | flops 128 | bytes 1024 | tf_op jit(solution)/shard_map/psum | solution.py:145
  323.0 4.2 %fusion.24 = bf16[128,2560]{1,0:T(8,128)(2,1)S(1)} fusion(bf16[1,1280,2560]{2,1,0:T(8,128)(2,1)} %param.31, f32[128,1280]{1,0:T(8,128)} %get-tuple-element.274, f32[128]{0:T(128)S(1)} %add_rsqrt_fusion, f32[1280]{0:T(1024)S(1)} %reduce.7), kind=kOutput, calls=%fused_computation.26 | convolution fusion | flops 839680000 | bytes 7869952 | tf_op jit(solution)/shard_map/dot_general | solution.py:147
  327.2 1.1 copy.99
  329.1 24.6 %reduce-scatter.14.cloned.1.call-done = bf16[640,128]{1,0:T(8,128)(2,1)} async-done(((bf16[2560,128]{1,0:T(8,128)(2,1)}), bf16[640,128]{1,0:T(8,128)(2,1)}) %reduce-scatter.14.cloned.1.call-update) | async-done | bytes 163856
  353.7 1.1 copy.100
  (176 shorter events, 20.9 us)
Async XLA Ops:
  6.5 31.3 %copy-start = (bf16[1,2560,256]{2,1,0:T(8,128)(2,1)S(1)}, bf16[1,2560,256]{2,1,0:T(8,128)(2,1)}, u32[]{:S(2)}) copy-start(bf16[1,2560,256]{2,1,0:T(8,128)(2,1)} %param.23) | copy-start | bytes 3932164
  6.5 26.2 %copy-start.18 = (f32[1,20]{1,0:T(1,128)S(1)}, f32[1,20]{1,0:T(1,128)}, u32[]{:S(2)}) copy-start(f32[1,20]{1,0:T(1,128)} %param.28) | copy-start | bytes 244
  6.5 23.3 %all-gather.11.cloned.1.call-start = ((), (), s32[]{:S(2)}) async-start(), calls=%async_computation.3 | async-start | bytes 1638400 | tf_op jit(solution)/shard_map/all_gather | solution.py:183
  7.3 74.9 %all-gather.13.cloned.1.call-start = ((), (), s32[]{:S(2)}) async-start(), calls=%async_computation.4 | async-start | bytes 1638400 | tf_op jit(solution)/shard_map/all_gather | solution.py:20
  29.8 4.0 %copy-start.1 = (bf16[2,128,2560]{2,1,0:T(8,128)(2,1)S(1)}, bf16[2,128,2560]{2,1,0:T(8,128)(2,1)}, u32[]{:S(2)}) copy-start(bf16[2,128,2560]{2,1,0:T(8,128)(2,1)} %all-gather.11.cloned.1.call-done) | copy-start | bytes 3932164
  31.2 6.6 %copy-start.21 = (f32[128]{0:T(128)}, f32[128]{0:T(128)S(1)}, u32[]{:S(2)}) copy-start(f32[128]{0:T(128)S(1)} %add_rsqrt_fusion.5) | copy-start | bytes 1540
  37.8 0.7 copy-start.11
  39.1 5.0 %collective-permute-start = (bf16[3,1536]{1,0:T(4,128)(2,1)}, bf16[3,1536]{1,0:T(4,128)(2,1)S(1)}, u32[]{:S(2)}, u32[]{:S(2)}) collective-permute-start(bf16[3,1536]{1,0:T(4,128)(2,1)} %pad_maximum_fusion), channel_id=1, source_target_pairs={{0,1},{1,2},{2,3},{4,5},{5,6},{6,7},{8,9},{9,10},{10,11},{12,13},{... | collective-permute-start | bytes 27656 | tf_op jit(solution)/shard_map/ppermute | solution.py:14
  43.7 1.4 copy-start.9
  46.3 2.4 copy-start.17
  46.3 2.4 copy-start.25
  48.7 78.0 %reduce-scatter.10.cloned.1.call-start = ((), (), s32[]{:S(2)}) async-start(), calls=%async_computation.7 | async-start | bytes 819200
  82.2 1.1 copy-start.12
  82.2 1.2 copy-start.15
  82.2 1.2 copy-start.31
  84.1 1.1 copy-start.22
  101.2 26.5 %slice-start = ((bf16[2,128,2560]{2,1,0:T(8,128)(2,1)}), bf16[1,128,2560]{2,1,0:T(8,128)(2,1)S(1)}, s32[]{:S(2)}) async-start(bf16[2,128,2560]{2,1,0:T(8,128)(2,1)} %all-gather.11.cloned.1.call-done), calls=%async_computation.10 | async-start | bytes 1310720 | tf_op jit(solution)/shard_map/slice | solution.py:190
  101.2 95.0 %all-gather.15.cloned.1.call-start = ((), (), s32[]{:S(2)}) async-start(), calls=%async_computation.5 | async-start | bytes 1638400 | tf_op jit(solution)/shard_map/all_gather | solution.py:20
  128.5 0.7 copy-start.6
  129.2 7.0 %collective-permute-start.1 = (bf16[128,640]{1,0:T(8,128)(2,1)}, bf16[128,640]{1,0:T(8,128)(2,1)S(1)}, u32[]{:S(2)}, u32[]{:S(2)}) collective-permute-start(bf16[128,640]{1,0:T(8,128)(2,1)} %get-tuple-element.249), channel_id=1, source_target_pairs={{0,16},{1,17},{2,18},{3,19},{4,20},{5,21},{6,22},{7,23},{8,24},{9,... | collective-permute-start | bytes 491528 | tf_op jit(solution)/shard_map/ppermute | solution.py:14
  143.4 4.5 %copy-start.4 = (bf16[128,2560]{1,0:T(8,128)(2,1)}, bf16[128,2560]{1,0:T(8,128)(2,1)S(1)}, u32[]{:S(2)}) copy-start(bf16[128,2560]{1,0:T(8,128)(2,1)S(1)} %get-tuple-element.247) | copy-start | bytes 1966084
  143.4 4.5 %copy-start.23 = (f32[128]{0:T(128)}, f32[128]{0:T(128)S(1)}, u32[]{:S(2)}) copy-start(f32[128]{0:T(128)S(1)} %add_rsqrt_fusion.3) | copy-start | bytes 1540
  143.9 4.1 %copy-start.27 = (bf16[1,2560,20]{1,2,0:T(8,128)(2,1)S(1)}, bf16[1,2560,20]{1,2,0:T(8,128)(2,1)}, u32[]{:S(2)}) copy-start(bf16[1,2560,20]{1,2,0:T(8,128)(2,1)} %param.24) | copy-start | bytes 307204
  143.9 4.1 %copy-start.29 = (f32[1,20]{1,0:T(1,128)S(1)}, f32[1,20]{1,0:T(1,128)}, u32[]{:S(2)}) copy-start(f32[1,20]{1,0:T(1,128)} %param.27) | copy-start | bytes 244
  147.9 6.1 %copy-start.10 = (bf16[128,1280]{1,0:T(8,128)(2,1)}, bf16[128,1280]{1,0:T(8,128)(2,1)S(1)}, u32[]{:S(2)}) copy-start(bf16[128,1280]{1,0:T(8,128)(2,1)S(1)} %fusion.30) | copy-start | bytes 983044
  149.9 5.2 %collective-permute-start.2 = (bf16[3,1536]{1,0:T(4,128)(2,1)}, bf16[3,1536]{1,0:T(4,128)(2,1)}, u32[]{:S(2)}, u32[]{:S(2)}) collective-permute-start(bf16[3,1536]{1,0:T(4,128)(2,1)} %pad_maximum_fusion.1), channel_id=1, source_target_pairs={{0,1},{1,2},{2,3},{4,5},{5,6},{6,7},{8,9},{9,10},{10,11},{12,13},{... | collective-permute-start | bytes 27656 | tf_op jit(solution)/shard_map/ppermute | solution.py:14
  155.1 2.6 copy-start.8
  159.0 2.2 copy-start.26
  161.2 83.6 %reduce-scatter.12.cloned.1.call-start = ((), (), s32[]{:S(2)}) async-start(), calls=%async_computation.8 | async-start | bytes 819200
  196.4 1.1 copy-start.13
  196.4 1.2 copy-start.16
  196.4 1.2 copy-start.32
  199.1 2.2 copy-start.5
  199.1 2.2 copy-start.24
  219.3 90.2 %all-gather.17.cloned.1.call-start = ((), (), s32[]{:S(2)}) async-start(), calls=%async_computation.6 | async-start | bytes 1638400 | tf_op jit(solution)/shard_map/all_gather | solution.py:20
  248.1 6.7 %collective-permute-start.3 = (bf16[128,640]{1,0:T(8,128)(2,1)S(1)}, bf16[128,640]{1,0:T(8,128)(2,1)S(1)}, u32[]{:S(2)}, u32[]{:S(2)}) collective-permute-start(bf16[128,640]{1,0:T(8,128)(2,1)S(1)} %get-tuple-element.243), channel_id=1, source_target_pairs={{0,16},{1,17},{2,18},{3,19},{4,20},{5,21},{6,22},{7,23},{8,24},{9,... | collective-permute-start | bytes 491528 | tf_op jit(solution)/shard_map/ppermute | solution.py:14
  262.0 4.5 %copy-start.2 = (bf16[128,2560]{1,0:T(8,128)(2,1)}, bf16[128,2560]{1,0:T(8,128)(2,1)S(1)}, u32[]{:S(2)}) copy-start(bf16[128,2560]{1,0:T(8,128)(2,1)S(1)} %get-tuple-element.241) | copy-start | bytes 1966084
  262.0 4.5 %copy-start.19 = (f32[128]{0:T(128)}, f32[128]{0:T(128)S(1)}, u32[]{:S(2)}) copy-start(f32[128]{0:T(128)S(1)} %add_rsqrt_fusion.1) | copy-start | bytes 1540
  262.4 4.1 %copy-start.28 = (bf16[1,2560,20]{1,2,0:T(8,128)(2,1)S(1)}, bf16[1,2560,20]{1,2,0:T(8,128)(2,1)}, u32[]{:S(2)}) copy-start(bf16[1,2560,20]{1,2,0:T(8,128)(2,1)} %param.24) | copy-start | bytes 307204
  262.4 4.1 %copy-start.30 = (f32[1,20]{1,0:T(1,128)S(1)}, f32[1,20]{1,0:T(1,128)}, u32[]{:S(2)}) copy-start(f32[1,20]{1,0:T(1,128)} %param.27) | copy-start | bytes 244
  267.4 4.8 %collective-permute-start.4 = (bf16[3,1536]{1,0:T(4,128)(2,1)S(1)}, bf16[3,1536]{1,0:T(4,128)(2,1)S(1)}, u32[]{:S(2)}, u32[]{:S(2)}) collective-permute-start(bf16[3,1536]{1,0:T(4,128)(2,1)S(1)} %pad_maximum_fusion.2), channel_id=1, source_target_pairs={{0,1},{1,2},{2,3},{4,5},{5,6},{6,7},{8,9},{9,10},{10,11},{12,13},{... | collective-permute-start | bytes 27656 | tf_op jit(solution)/shard_map/ppermute | solution.py:14
  274.1 79.6 %reduce-scatter.14.cloned.1.call-start = ((), (), s32[]{:S(2)}) async-start(), calls=%async_computation.9 | async-start | bytes 819200
  309.6 1.0 copy-start.14
  309.6 1.0 copy-start.33
  311.2 1.1 copy-start.3
  311.2 1.1 copy-start.20
  327.2 1.1 copy-start.7
Sparse Core Ops, SparseCore 0:
  8.9 20.8 all-gather.10
  48.8 33.3 all-gather.12
  101.4 25.1 reduce-scatter.9
  161.3 34.9 all-gather.14
  219.5 25.2 reduce-scatter.11
  274.2 35.2 all-gather.16
  328.5 25.1 reduce-scatter.13
where the time goes:
time: 364 us; the launch traced here: 362 us
  waiting for transfers between devices  167 us (46%)
  blocking collectives  66.3 us (18%)
  matrix products  51.1 us (14%)
  local copies, waits for them, and re-layouts  31.4 us (9%)
  starting transfers between devices  17.7 us (5%)
  other arithmetic  14.7 us (4%)
  between operations  14.3 us (4%)
    unnamed x10, waiting for transfers between devices  75.1 us
    all_gather x3, waiting for transfers between devices, prefix(): lax.all_gather(a.astype(kind), axis)  63.2 us
    all_gather x3, blocking collectives, prefix(): lax.all_gather(a.astype(kind), axis)  35 us
    all_gather x1, waiting for transfers between devices, shards(): all_tokens = lax.all_gather(tokens, 'tensor', axis=2, tiled=True)  20.2 us
    ppermute x5, starting transfers between devices, shifted(): lax.ppermute(value, axis, [(source, source + steps) for source in range(f...  17.5 us
    psum x3, blocking collectives, mixer(): squares = lax.psum(jnp.sum(gated * gated, axis=1), 'tensor')  17.5 us
    dot_general x3, matrix products, mixer(): jnp.dot(normed_in, gate_weight, preferred_element_type=jnp.float32)  14.9 us
    all_gather x2, blocking collectives, shards(): incoming = lax.all_gather(carried, 'tensor', axis=1, tiled=True)  13.8 us
  transfers between devices with their start and end apart: 12, of which 11 were waited for; matrix products, arithmetic and copies ran while one was open for 3% of the time, Pallas kernels for 0%

commit v1 on v0

--- a/solution.py
+++ b/solution.py
@@ -6,6 +6,17 @@
 BLOCK = 128
 INNER = 5120
 EPS = 1e-05
+
+
+def pass_along(array, name, d):
+    size = lax.axis_size(name)
+    right = [(i, (i + 1) % size) for i in range(size)]
+    pieces = [array]
+    for far in range(1, size):
+        pieces = [lax.ppermute(pieces[0], name, right), *pieces]
+    whole = jnp.concatenate(pieces, axis=d)
+    shift = (lax.axis_index(name) + 1) * pieces[-1].shape[d]
+    return jnp.roll(whole, shift, axis=d)
 
 
 def shifted(value, axis, steps):
@@ -180,7 +191,7 @@
     section = lax.axis_index("pipe")
     share = lax.axis_size("tensor")
     member = lax.axis_index("tensor")
-    all_tokens = lax.all_gather(tokens, "tensor", axis=2, tiled=True)
+    all_tokens = pass_along(tokens, "tensor", 2)
     micro_count, rows, width = all_tokens.shape
     narrow = width // share
     outputs = jnp.zeros((micro_count, rows, narrow), jnp.bfloat16)

time: 364 us -> 350 us (0.962)
  local copies, waits for them, and re-layouts: 31.4 us -> 23.9 us
    all_gather x1 -> x0, waiting for transfers between devices: 20.2 us -> none  [shards(): all_tokens = lax.all_gather(tokens, 'tensor', axis=2, tiled=True)]
    ppermute x0 -> x3, waiting for transfers between devices: none -> 17.6 us  [pass_along(): pieces = [lax.ppermute(pieces[0], name, right), *pieces]]
    unnamed x78 -> x71, local copies, waits for them, and re-layouts: 12.8 us -> 12 us
    unnamed x10 -> x9, waiting for transfers between devices: 75.1 us -> 75.3 us
  transfers between devices with their start and end apart: 12 -> 14, of which waited for: 11 -> 12; matrix products, arithmetic and copies ran while one was open for 3% -> 3% of each run, Pallas kernels for 0% -> 0%
where the time goes in v1:
time: 350 us; the launch traced here: 349 us
  waiting for transfers between devices  167 us (48%)
  blocking collectives  64 us (18%)
  matrix products  49 us (14%)
  local copies, waits for them, and re-layouts  23.9 us (7%)
  starting transfers between devices  18.7 us (5%)
  between operations  14.3 us (4%)
  other arithmetic  11.5 us (3%)
    unnamed x9, waiting for transfers between devices  75.3 us
    all_gather x3, waiting for transfers between devices, prefix(): lax.all_gather(a.astype(kind), axis)  66.5 us
    all_gather x3, blocking collectives, prefix(): lax.all_gather(a.astype(kind), axis)  32.7 us
    ppermute x5, starting transfers between devices, shifted(): lax.ppermute(value, axis, [(source, source + steps) for source in range(f...  17.9 us
    ppermute x3, waiting for transfers between devices, pass_along(): pieces = [lax.ppermute(pieces[0], name, right), *pieces]  17.6 us
    psum x3, blocking collectives, mixer(): squares = lax.psum(jnp.sum(gated * gated, axis=1), 'tensor')  17.5 us
    dot_general x3, matrix products, mixer(): jnp.dot(normed_in, gate_weight, preferred_element_type=jnp.float32)  14.4 us
    all_gather x2, blocking collectives, shards(): incoming = lax.all_gather(carried, 'tensor', axis=1, tiled=True)  13.8 us
  transfers between devices with their start and end apart: 14, of which 12 were waited for; matrix products, arithmetic and copies ran while one was open for 3% of the time, Pallas kernels for 0%

profile of v1, /device:TPU:0, one launch (start us, length us, event | category | flops | bytes accessed | tf_op | source)
XLA Modules:
  0.0 348.7 jit_solution(3381046231970159478)
XLA Ops:
  7.0 6.9 %collective-permute-done = bf16[2,128,640]{2,1,0:T(8,128)(2,1)S(1)} collective-permute-done((bf16[2,128,640]{2,1,0:T(8,128)(2,1)}, bf16[2,128,640]{2,1,0:T(8,128)(2,1)S(1)}, u32[]{:S(2)}, u32[]{:S(2)}) %collective-permute-start) | collective-permute-done | bytes 327712 | tf_op jit(solution)/shard_map/ppermute | solution.py:16
  14.0 0.7 reduce.3
  14.7 5.8 %collective-permute-done.1 = bf16[2,128,640]{2,1,0:T(8,128)(2,1)S(1)} collective-permute-done((bf16[2,128,640]{2,1,0:T(8,128)(2,1)S(1)}, bf16[2,128,640]{2,1,0:T(8,128)(2,1)S(1)}, u32[]{:S(2)}, u32[]{:S(2)}) %collective-permute-start.1) | collective-permute-done | bytes 327712 | tf_op jit(solution)/shard_map/ppermute | solution.py:16
  20.5 0.8 slice_reduce_fusion.4
  21.3 0.8 fusion.201
  22.1 4.9 %collective-permute-done.2 = bf16[2,128,640]{2,1,0:T(8,128)(2,1)S(1)} collective-permute-done((bf16[2,128,640]{2,1,0:T(8,128)(2,1)S(1)}, bf16[2,128,640]{2,1,0:T(8,128)(2,1)S(1)}, u32[]{:S(2)}, u32[]{:S(2)}) %collective-permute-start.2) | collective-permute-done | bytes 327712 | tf_op jit(solution)/shard_map/ppermute | solution.py:16
  27.9 1.1 copy-done.1
  29.9 1.6 fusion.81
  31.5 4.2 %fusion.27 = bf16[128,1280]{1,0:T(8,128)(2,1)S(1)} fusion(bf16[1,2560,1280]{2,1,0:T(8,128)(2,1)} %param.22, f32[2560]{0:T(1024)S(1)} %reduce.3, f32[128]{0:T(128)S(1)} %add_rsqrt_fusion.5, bf16[2,128,5120]{2,1,0:T(8,128)(2,1)} %copy-done.1, s32[]{:T(128)S(6)} %select_n.106), kind=kOutput, calls=%fused_computation.27 | convolution fusion | flops 840335360 | bytes 7547396 | tf_op jit(solution)/shard_map/dot_general | solution.py:91
  35.8 4.2 %collective-permute-start.3 = (bf16[3,1536]{1,0:T(4,128)(2,1)S(1)}, bf16[3,1536]{1,0:T(4,128)(2,1)S(1)}, u32[]{:S(2)}, u32[]{:S(2)}) collective-permute-start(bf16[3,1536]{1,0:T(4,128)(2,1)S(1)} %pad_maximum_fusion), channel_id=1, source_target_pairs={{0,1},{1,2},{2,3},{4,5},{5,6},{6,7},{8,9},{9,10},{10,11},{12,13},{... | collective-permute-start | bytes 27656 | tf_op jit(solution)/shard_map/ppermute | solution.py:25
  40.4 1.0 collective-permute-done.3
  42.3 1.0 fusion.78
  43.4 11.9 %all-gather = bf16[4,1,20]{2,1,0:T(2,128)(2,1)S(1)} all-gather(bf16[1,1,20]{2,1,0:T(2,128)(2,1)S(1)} %get-tuple-element.257), channel_id=2, replica_groups=mesh['pipe'=2,'tensor'=4,'seq'=4] {'seq'}, dimensions={0}, use_global_device_ids=true | all-gather | bytes 200 | tf_op jit(solution)/shard_map/all_gather | solution.py:31
  55.9 22.1 %all-gather.10.cloned.1.call-done = bf16[80,64,128]{2,1,0:T(8,128)(2,1)} async-done(((bf16[20,64,128]{2,1,0:T(8,128)(2,1)}), bf16[80,64,128]{2,1,0:T(8,128)(2,1)}) %all-gather.10.cloned.1.call-update) | async-done | bytes 1310736 | tf_op jit(solution)/shard_map/all_gather | solution.py:31
  78.7 0.7 fusion.77
  79.4 1.1 copy.76
  80.4 4.4 %multiply_reduce_fusion.2 = (f32[128]{0:T(128)S(1)}, f32[128,1280]{1,0:T(8,128)S(1)}) fusion(f32[128,1280]{1,0:T(8,128)} %copy.76, bf16[1,2560,1280]{2,1,0:T(8,128)(2,1)} %param.21, f32[2560]{0:T(1024)S(1)} %reduce.3, f32[128]{0:T(128)S(1)} %add_rsqrt_fusion.5, bf16[2,128,5120]{2,1,0:T(8,128)(2,1)} %copy-done.1, s32[]{:T(128)S(6)} %select_n.106), kind=kOutput, calls=%fused_computation.132 | convolution fusion | flops 841645952 | bytes 8530948 | tf_op jit(solution)/shard_map/dot_general | solution.py:88
  84.9 5.9 %psum.21 = f32[128]{0:T(128)S(1)} all-reduce(f32[128]{0:T(128)S(1)} %get-tuple-element.269), channel_id=1, replica_groups=mesh['pipe'=2,'tensor'=4,'seq'=4] {'tensor'}, use_global_device_ids=true, to_apply=%region_5.6 | all-reduce | flops 128 | bytes 1024 | tf_op jit(solution)/shard_map/psum | solution.py:156
  90.8 3.9 %fusion.18 = bf16[128,2560]{1,0:T(8,128)(2,1)S(1)} fusion(bf16[1,1280,2560]{2,1,0:T(8,128)(2,1)} %param.31, f32[128,1280]{1,0:T(8,128)S(1)} %get-tuple-element.270, f32[1280]{0:T(1024)S(1)} %reduce.7, f32[128]{0:T(128)S(1)} %add_rsqrt_fusion.4), kind=kOutput, calls=%fused_computation.24 | convolution fusion | flops 839680000 | bytes 7869952 | tf_op jit(solution)/shard_map/dot_general | solution.py:158
  94.7 1.1 copy.95
  95.9 25.3 %reduce-scatter.10.cloned.1.call-done = bf16[640,128]{1,0:T(8,128)(2,1)} async-done(((bf16[2560,128]{1,0:T(8,128)(2,1)}), bf16[640,128]{1,0:T(8,128)(2,1)}) %reduce-scatter.10.cloned.1.call-update) | async-done | bytes 163856
  121.2 1.1 copy.96
  122.3 1.1 bitcast_dynamic-update-slice_fusion.1
  123.4 3.4 collective-permute-start.4
  126.8 3.3 collective-permute-done.4
  130.0 6.9 %all_gather.32 = bf16[128,2560]{1,0:T(8,128)(2,1)S(1)} all-gather(bf16[128,640]{1,0:T(8,128)(2,1)S(1)} %collective-permute-done.4), channel_id=1, replica_groups=mesh['pipe'=2,'tensor'=4,'seq'=4] {'tensor'}, dimensions={1}, use_global_device_ids=true | all-gather | bytes 819200 | tf_op jit(solution)/shard_map/all_gather | solution.py:205
  136.9 1.6 fusion.57
  139.0 4.0 %fusion.30 = bf16[128,1280]{1,0:T(8,128)(2,1)S(1)} fusion(bf16[1,2560,1280]{2,1,0:T(8,128)(2,1)} %param.22, bf16[128,2560]{1,0:T(8,128)(2,1)S(1)} %get-tuple-element.247, f32[2560]{0:T(1024)S(1)} %reduce.3, f32[128]{0:T(128)S(1)} %add_rsqrt_fusion.3), kind=kOutput, calls=%fused_computation.28 | convolution fusion | flops 840335360 | bytes 7547392 | tf_op jit(solution)/shard_map/dot_general | solution.py:91
  144.4 3.6 %collective-permute-start.5 = (bf16[3,1536]{1,0:T(4,128)(2,1)S(1)}, bf16[3,1536]{1,0:T(4,128)(2,1)S(1)}, u32[]{:S(2)}, u32[]{:S(2)}) collective-permute-start(bf16[3,1536]{1,0:T(4,128)(2,1)S(1)} %pad_maximum_fusion.1), channel_id=1, source_target_pairs={{0,1},{1,2},{2,3},{4,5},{5,6},{6,7},{8,9},{9,10},{10,11},{12,13},{... | collective-permute-start | bytes 27656 | tf_op jit(solution)/shard_map/ppermute | solution.py:25
  148.6 1.1 copy.82
  150.0 0.8 copy-done.3
  151.5 1.0 fusion.79
  152.5 10.3 %all-gather.2 = bf16[4,1,20]{2,1,0:T(2,128)(2,1)S(1)} all-gather(bf16[1,1,20]{2,1,0:T(2,128)(2,1)S(1)} %copy-done.17), channel_id=4, replica_groups=mesh['pipe'=2,'tensor'=4,'seq'=4] {'seq'}, dimensions={0}, use_global_device_ids=true | all-gather | bytes 200 | tf_op jit(solution)/shard_map/all_gather | solution.py:31
  162.9 1.0 copy.84
  164.3 22.2 %all-gather.12.cloned.1.call-done = bf16[80,64,128]{2,1,0:T(8,128)(2,1)} async-done(((bf16[20,64,128]{2,1,0:T(8,128)(2,1)}), bf16[80,64,128]{2,1,0:T(8,128)(2,1)}) %all-gather.12.cloned.1.call-update) | async-done | bytes 1310736 | tf_op jit(solution)/shard_map/all_gather | solution.py:31
  188.4 1.1 copy.85
  189.5 5.0 %multiply_reduce_fusion.1 = (f32[128]{0:T(128)S(1)}, f32[128,1280]{1,0:T(8,128)}) fusion(f32[128,1280]{1,0:T(8,128)} %copy.85, bf16[1,2560,1280]{2,1,0:T(8,128)(2,1)} %param.21, bf16[128,2560]{1,0:T(8,128)(2,1)S(1)} %get-tuple-element.247, f32[2560]{0:T(1024)S(1)} %reduce.3, f32[128]{0:T(128)S(1)} %copy-done.13), kind=kOutput, calls=%fused_computation.123 | convolution fusion | flops 841645952 | bytes 8530944 | tf_op jit(solution)/shard_map/dot_general | solution.py:88
  194.5 5.8 %psum.22 = f32[128]{0:T(128)S(1)} all-reduce(f32[128]{0:T(128)S(1)} %get-tuple-element.271), channel_id=1, replica_groups=mesh['pipe'=2,'tensor'=4,'seq'=4] {'tensor'}, use_global_device_ids=true, to_apply=%region_12.13 | all-reduce | flops 128 | bytes 1024 | tf_op jit(solution)/shard_map/psum | solution.py:156
  200.3 4.2 %fusion.21 = bf16[128,2560]{1,0:T(8,128)(2,1)S(1)} fusion(bf16[1,1280,2560]{2,1,0:T(8,128)(2,1)} %param.31, f32[128,1280]{1,0:T(8,128)} %get-tuple-element.272, f32[128]{0:T(128)S(1)} %add_rsqrt_fusion.2, f32[1280]{0:T(1024)S(1)} %reduce.7), kind=kOutput, calls=%fused_computation.25 | convolution fusion | flops 839680000 | bytes 7869952 | tf_op jit(solution)/shard_map/dot_general | solution.py:158
  204.5 1.1 copy.97
  205.7 25.3 %reduce-scatter.12.cloned.1.call-done = bf16[640,128]{1,0:T(8,128)(2,1)} async-done(((bf16[2560,128]{1,0:T(8,128)(2,1)}), bf16[640,128]{1,0:T(8,128)(2,1)}) %reduce-scatter.12.cloned.1.call-update) | async-done | bytes 163856
  231.0 1.1 copy.98
  232.1 3.4 collective-permute-start.6
  235.5 3.3 collective-permute-done.6
  238.8 6.9 %all_gather.35 = bf16[128,2560]{1,0:T(8,128)(2,1)S(1)} all-gather(bf16[128,640]{1,0:T(8,128)(2,1)S(1)} %collective-permute-done.6), channel_id=1, replica_groups=mesh['pipe'=2,'tensor'=4,'seq'=4] {'tensor'}, dimensions={1}, use_global_device_ids=true | all-gather | bytes 819200 | tf_op jit(solution)/shard_map/all_gather | solution.py:205
  245.7 1.6 fusion.60
  247.8 4.0 %fusion.33 = bf16[128,1280]{1,0:T(8,128)(2,1)S(1)} fusion(bf16[1,2560,1280]{2,1,0:T(8,128)(2,1)} %param.22, bf16[128,2560]{1,0:T(8,128)(2,1)S(1)} %get-tuple-element.241, f32[128]{0:T(128)S(1)} %add_rsqrt_fusion.1, f32[2560]{0:T(1024)S(1)} %reduce.3), kind=kOutput, calls=%fused_computation.29 | convolution fusion | flops 840335360 | bytes 7547392 | tf_op jit(solution)/shard_map/dot_general | solution.py:91
  253.2 3.4 collective-permute-start.7
  257.3 1.1 copy.91
  258.6 0.8 copy-done.2
  260.2 1.0 fusion.80
  261.2 10.5 %all-gather.4 = bf16[4,1,20]{2,1,0:T(2,128)(2,1)S(1)} all-gather(bf16[1,1,20]{2,1,0:T(2,128)(2,1)S(1)} %copy-done.16), channel_id=6, replica_groups=mesh['pipe'=2,'tensor'=4,'seq'=4] {'seq'}, dimensions={0}, use_global_device_ids=true | all-gather | bytes 200 | tf_op jit(solution)/shard_map/all_gather | solution.py:31
  271.8 1.1 copy.93
  273.2 22.2 %all-gather.14.cloned.1.call-done = bf16[80,64,128]{2,1,0:T(8,128)(2,1)} async-done(((bf16[20,64,128]{2,1,0:T(8,128)(2,1)}), bf16[80,64,128]{2,1,0:T(8,128)(2,1)}) %all-gather.14.cloned.1.call-update) | async-done | bytes 1310736 | tf_op jit(solution)/shard_map/all_gather | solution.py:31
  296.8 0.7 fusion.75
  297.5 1.1 copy.94
  298.5 5.0 %multiply_reduce_fusion = (f32[128]{0:T(128)S(1)}, f32[128,1280]{1,0:T(8,128)}) fusion(f32[128,1280]{1,0:T(8,128)} %copy.94, bf16[1,2560,1280]{2,1,0:T(8,128)(2,1)} %param.21, bf16[128,2560]{1,0:T(8,128)(2,1)S(1)} %get-tuple-element.241, f32[128]{0:T(128)S(1)} %copy-done.11, f32[2560]{0:T(1024)S(1)} %reduce.3), kind=kOutput, calls=%fused_computation.114 | convolution fusion | flops 841645952 | bytes 8530944 | tf_op jit(solution)/shard_map/dot_general | solution.py:88
  303.5 5.8 %psum.23 = f32[128]{0:T(128)S(1)} all-reduce(f32[128]{0:T(128)S(1)} %get-tuple-element.273), channel_id=1, replica_groups=mesh['pipe'=2,'tensor'=4,'seq'=4] {'tensor'}, use_global_device_ids=true, to_apply=%region_19.20 | all-reduce | flops 128 | bytes 1024 | tf_op jit(solution)/shard_map/psum | solution.py:156
  309.4 4.2 %fusion.24 = bf16[128,2560]{1,0:T(8,128)(2,1)S(1)} fusion(bf16[1,1280,2560]{2,1,0:T(8,128)(2,1)} %param.31, f32[128,1280]{1,0:T(8,128)} %get-tuple-element.274, f32[128]{0:T(128)S(1)} %add_rsqrt_fusion, f32[1280]{0:T(1024)S(1)} %reduce.7), kind=kOutput, calls=%fused_computation.26 | convolution fusion | flops 839680000 | bytes 7869952 | tf_op jit(solution)/shard_map/dot_general | solution.py:158
  313.5 1.1 copy.99
  314.7 0.7 copy.137
  315.4 24.6 %reduce-scatter.14.cloned.1.call-done = bf16[640,128]{1,0:T(8,128)(2,1)} async-done(((bf16[2560,128]{1,0:T(8,128)(2,1)}), bf16[640,128]{1,0:T(8,128)(2,1)}) %reduce-scatter.14.cloned.1.call-update) | async-done | bytes 163856
  340.0 1.1 copy.100
  341.1 0.7 fusion.136
  (171 shorter events, 16.0 us)
Async XLA Ops:
  6.5 23.4 %copy-start = (bf16[1,2560,256]{2,1,0:T(8,128)(2,1)S(1)}, bf16[1,2560,256]{2,1,0:T(8,128)(2,1)}, u32[]{:S(2)}) copy-start(bf16[1,2560,256]{2,1,0:T(8,128)(2,1)} %param.23) | copy-start | bytes 3932164
  6.5 20.6 %copy-start.4 = (bf16[2,128,640]{2,1,0:T(8,128)(2,1)S(1)}, bf16[2,128,640]{2,1,0:T(8,128)(2,1)}, u32[]{:S(2)}) copy-start(bf16[2,128,640]{2,1,0:T(8,128)(2,1)} %param.19) | copy-start | bytes 983044
  6.5 71.4 %all-gather.10.cloned.1.call-start = ((), (), s32[]{:S(2)}) async-start(), calls=%async_computation.3 | async-start | bytes 1638400 | tf_op jit(solution)/shard_map/all_gather | solution.py:31
  6.5 7.4 %collective-permute-start = (bf16[2,128,640]{2,1,0:T(8,128)(2,1)}, bf16[2,128,640]{2,1,0:T(8,128)(2,1)S(1)}, u32[]{:S(2)}, u32[]{:S(2)}) collective-permute-start(bf16[2,128,640]{2,1,0:T(8,128)(2,1)} %param.19), channel_id=1, source_target_pairs={{0,4},{4,8},{8,12},{12,0},{1,5},{5,9},{9,13},{13,1},{2,6},{6,10},{... | collective-permute-start | bytes 983048 | tf_op jit(solution)/shard_map/ppermute | solution.py:16
  14.0 6.5 %collective-permute-start.1 = (bf16[2,128,640]{2,1,0:T(8,128)(2,1)S(1)}, bf16[2,128,640]{2,1,0:T(8,128)(2,1)S(1)}, u32[]{:S(2)}, u32[]{:S(2)}) collective-permute-start(bf16[2,128,640]{2,1,0:T(8,128)(2,1)S(1)} %collective-permute-done), channel_id=1, source_target_pairs={{0,4},{4,8},{8,12},{12,0},{1,5},{5,9},{9,13},{13,1},{2,6},{6,10},{... | collective-permute-start | bytes 983048 | tf_op jit(solution)/shard_map/ppermute | solution.py:16
  20.5 6.5 %collective-permute-start.2 = (bf16[2,128,640]{2,1,0:T(8,128)(2,1)S(1)}, bf16[2,128,640]{2,1,0:T(8,128)(2,1)S(1)}, u32[]{:S(2)}, u32[]{:S(2)}) collective-permute-start(bf16[2,128,640]{2,1,0:T(8,128)(2,1)S(1)} %collective-permute-done.1), channel_id=1, source_target_pairs={{0,4},{4,8},{8,12},{12,0},{1,5},{5,9},{9,13},{13,1},{2,6},{6,10},{... | collective-permute-start | bytes 983048 | tf_op jit(solution)/shard_map/ppermute | solution.py:16
  27.3 1.7 copy-start.18
  27.3 1.7 copy-start.21
  27.4 2.1 copy-start.8
  27.5 1.5 copy-start.1
  35.8 5.6 %collective-permute-start.3 = (bf16[3,1536]{1,0:T(4,128)(2,1)S(1)}, bf16[3,1536]{1,0:T(4,128)(2,1)S(1)}, u32[]{:S(2)}, u32[]{:S(2)}) collective-permute-start(bf16[3,1536]{1,0:T(4,128)(2,1)S(1)} %pad_maximum_fusion), channel_id=1, source_target_pairs={{0,1},{1,2},{2,3},{4,5},{5,6},{6,7},{8,9},{9,10},{10,11},{12,13},{... | collective-permute-start | bytes 27656 | tf_op jit(solution)/shard_map/ppermute | solution.py:25
  42.0 1.4 copy-start.7
  43.3 77.9 %reduce-scatter.10.cloned.1.call-start = ((), (), s32[]{:S(2)}) async-start(), calls=%async_computation.6 | async-start | bytes 819200
  78.0 0.7 copy-start.24
  95.8 90.7 %all-gather.12.cloned.1.call-start = ((), (), s32[]{:S(2)}) async-start(), calls=%async_computation.4 | async-start | bytes 1638400 | tf_op jit(solution)/shard_map/all_gather | solution.py:31
  123.4 6.7 %collective-permute-start.4 = (bf16[128,640]{1,0:T(8,128)(2,1)S(1)}, bf16[128,640]{1,0:T(8,128)(2,1)S(1)}, u32[]{:S(2)}, u32[]{:S(2)}) collective-permute-start(bf16[128,640]{1,0:T(8,128)(2,1)S(1)} %get-tuple-element.249), channel_id=1, source_target_pairs={{0,16},{1,17},{2,18},{3,19},{4,20},{5,21},{6,22},{7,23},{8,24},{9,... | collective-permute-start | bytes 491528 | tf_op jit(solution)/shard_map/ppermute | solution.py:25
  138.5 4.4 %copy-start.12 = (f32[128]{0:T(128)}, f32[128]{0:T(128)S(1)}, u32[]{:S(2)}) copy-start(f32[128]{0:T(128)S(1)} %add_rsqrt_fusion.3) | copy-start | bytes 1540
  139.0 4.0 %copy-start.19 = (bf16[1,2560,20]{1,2,0:T(8,128)(2,1)S(1)}, bf16[1,2560,20]{1,2,0:T(8,128)(2,1)}, u32[]{:S(2)}) copy-start(bf16[1,2560,20]{1,2,0:T(8,128)(2,1)} %param.24) | copy-start | bytes 307204
  139.0 4.0 %copy-start.22 = (f32[1,20]{1,0:T(1,128)S(1)}, f32[1,20]{1,0:T(1,128)}, u32[]{:S(2)}) copy-start(f32[1,20]{1,0:T(1,128)} %param.27) | copy-start | bytes 244
  144.4 5.3 %collective-permute-start.5 = (bf16[3,1536]{1,0:T(4,128)(2,1)S(1)}, bf16[3,1536]{1,0:T(4,128)(2,1)S(1)}, u32[]{:S(2)}, u32[]{:S(2)}) collective-permute-start(bf16[3,1536]{1,0:T(4,128)(2,1)S(1)} %pad_maximum_fusion.1), channel_id=1, source_target_pairs={{0,1},{1,2},{2,3},{4,5},{5,6},{6,7},{8,9},{9,10},{10,11},{12,13},{... | collective-permute-start | bytes 27656 | tf_op jit(solution)/shard_map/ppermute | solution.py:25
  149.7 1.1 copy-start.3
  150.8 0.7 copy-start.15
  151.3 1.3 copy-start.17
  152.5 78.5 %reduce-scatter.12.cloned.1.call-start = ((), (), s32[]{:S(2)}) async-start(), calls=%async_computation.7 | async-start | bytes 819200
  186.6 1.1 copy-start.6
  186.6 1.1 copy-start.25
  188.4 1.1 copy-start.13
  205.6 89.8 %all-gather.14.cloned.1.call-start = ((), (), s32[]{:S(2)}) async-start(), calls=%async_computation.5 | async-start | bytes 1638400 | tf_op jit(solution)/shard_map/all_gather | solution.py:31
  232.1 6.7 %collective-permute-start.6 = (bf16[128,640]{1,0:T(8,128)(2,1)S(1)}, bf16[128,640]{1,0:T(8,128)(2,1)S(1)}, u32[]{:S(2)}, u32[]{:S(2)}) collective-permute-start(bf16[128,640]{1,0:T(8,128)(2,1)S(1)} %get-tuple-element.243), channel_id=1, source_target_pairs={{0,16},{1,17},{2,18},{3,19},{4,20},{5,21},{6,22},{7,23},{8,24},{9,... | collective-permute-start | bytes 491528 | tf_op jit(solution)/shard_map/ppermute | solution.py:25
  247.3 4.4 %copy-start.10 = (f32[128]{0:T(128)}, f32[128]{0:T(128)S(1)}, u32[]{:S(2)}) copy-start(f32[128]{0:T(128)S(1)} %add_rsqrt_fusion.1) | copy-start | bytes 1540
  247.7 4.0 %copy-start.20 = (bf16[1,2560,20]{1,2,0:T(8,128)(2,1)S(1)}, bf16[1,2560,20]{1,2,0:T(8,128)(2,1)}, u32[]{:S(2)}) copy-start(bf16[1,2560,20]{1,2,0:T(8,128)(2,1)} %param.24) | copy-start | bytes 307204
  247.7 4.0 %copy-start.23 = (f32[1,20]{1,0:T(1,128)S(1)}, f32[1,20]{1,0:T(1,128)}, u32[]{:S(2)}) copy-start(f32[1,20]{1,0:T(1,128)} %param.27) | copy-start | bytes 244
  247.7 4.4 %copy-start.9 = (f32[1,20]{1,0:T(1,128)S(1)}, f32[1,20]{1,0:T(1,128)}, u32[]{:S(2)}) copy-start(f32[1,20]{1,0:T(1,128)} %param.28) | copy-start | bytes 244
  253.2 5.1 %collective-permute-start.7 = (bf16[3,1536]{1,0:T(4,128)(2,1)S(1)}, bf16[3,1536]{1,0:T(4,128)(2,1)S(1)}, u32[]{:S(2)}, u32[]{:S(2)}) collective-permute-start(bf16[3,1536]{1,0:T(4,128)(2,1)S(1)} %pad_maximum_fusion.2), channel_id=1, source_target_pairs={{0,1},{1,2},{2,3},{4,5},{5,6},{6,7},{8,9},{9,10},{10,11},{12,13},{... | collective-permute-start | bytes 27656 | tf_op jit(solution)/shard_map/ppermute | solution.py:25
  258.4 1.1 copy-start.2
  259.5 0.7 copy-start.14
  259.9 1.3 copy-start.16
  261.1 78.9 %reduce-scatter.14.cloned.1.call-start = ((), (), s32[]{:S(2)}) async-start(), calls=%async_computation.8 | async-start | bytes 819200
  295.7 1.1 copy-start.5
  295.7 1.1 copy-start.26
  297.5 1.1 copy-start.11
Sparse Core Ops, SparseCore 0:
  43.4 34.4 all-gather.9
  96.0 25.1 reduce-scatter.9
  152.6 33.8 all-gather.11
  205.7 25.1 reduce-scatter.11
  261.3 34.0 all-gather.13
  314.8 25.1 reduce-scatter.13
